TPU v7x, 32 devices: a whole 2x2x4 slice. The times are simulated.
32 devices in a mesh: py: 4 (over y, core), pz: 8 (over z, x).
Axes of the slice: x: 2, y: 2, z: 4, core: 2. Of those that a mesh axis runs over, the one named last changes fastest.
Arguments:
- wavefunctions: float32 [2, 8, 128, 128, 128], P(None, None, 'pz', 'py'), may hold values from -6 to 6
- potential: float32 [128, 128, 128], P('pz', 'py'), may hold values from -4 to 4
- cutoff_sq: int32 [1], replicated, may hold values from 2304 to 4096
- locked_mask: int32 [8], replicated, may hold values 0 or 1
Outputs:
- applied: float32 [2, 8, 128, 128, 128], P(None, None, 'pz', 'py')
- rayleigh: float32 [8], replicated
- residual_norm: float32 [8], replicated
All inputs are finite; a program needn't handle non-finite values.
Results may differ from a plain program's by a relative error of at most 0.00005.
Values sent between devices are 32-bit elements; how exact they have to be, the bound alone decides.
A program may use at most 64 MiB of HBM per device.

v0:
```python
import math

import jax
import jax.numpy as jnp
from jax import lax
from jax.sharding import PartitionSpec as P


def make_tables(length, inverse):
    counter = jnp.arange(length, dtype=jnp.int32)
    phase = counter[:, None] * counter[None, :] % length
    angle = 2.0 * math.pi / length * phase.astype(jnp.float32)
    if inverse:
        return (jnp.cos(angle) / length, jnp.sin(angle) / length)
    return (jnp.cos(angle), -jnp.sin(angle))


def transform_axis(field, axis, tables):
    cosines, sines = tables
    letters = "abcdefgh"[: field.ndim - 1]
    place = axis - 1
    source = letters[:place] + "n" + letters[place + 1 :]
    target = letters[:place] + "k" + letters[place + 1 :]
    form = source + ",kn->" + target
    real_part = field[0]
    imag_part = field[1]
    high = lax.Precision.HIGHEST
    out_real = jnp.einsum(form, real_part, cosines, precision=high) - jnp.einsum(
        form, imag_part, sines, precision=high
    )
    out_imag = jnp.einsum(form, real_part, sines, precision=high) + jnp.einsum(
        form, imag_part, cosines, precision=high
    )
    return jnp.stack([out_real, out_imag])


def signed_square(counter, length):
    signed = jnp.where(counter < length // 2, counter, counter - length)
    return signed * signed


def kinetic_table(first_sq, second_sq, third_sq, cutoff_sq, length):
    total = first_sq[:, None, None] + second_sq[None, :, None] + third_sq[None, None, :]
    keep = (total <= cutoff_sq[0]).astype(jnp.float32)
    return 0.5 * (math.pi / length) ** 2 * total.astype(jnp.float32) * keep


def slab_kinetic(field, cutoff_sq, forward, inverse):
    parts, bands, rows_z, rows_y, length = field.shape
    size_y = lax.axis_size("py")
    size_z = lax.axis_size("pz")
    along_x = transform_axis(field, 4, forward)
    flat = jnp.moveaxis(along_x, 1, 3).reshape(parts, rows_z, rows_y, bands * length)
    planes = lax.all_to_all(
        lax.all_to_all(flat, "py", split_axis=3, concat_axis=2, tiled=True),
        "pz",
        split_axis=3,
        concat_axis=1,
        tiled=True,
    )
    width = planes.shape[3]
    start = lax.axis_index("py") * (bands * length // size_y) + lax.axis_index("pz") * width
    column = start + jnp.arange(width, dtype=jnp.int32)
    full_counter = jnp.arange(length, dtype=jnp.int32)
    full_sq = signed_square(full_counter, length)
    kinetic = kinetic_table(
        full_sq, full_sq, signed_square(column % length, length), cutoff_sq, length
    )
    spectrum = transform_axis(transform_axis(planes, 1, forward), 2, forward) * kinetic
    spatial = transform_axis(transform_axis(spectrum, 2, inverse), 1, inverse)
    returned = lax.all_to_all(
        lax.all_to_all(spatial, "py", split_axis=2, concat_axis=3, tiled=True),
        "pz",
        split_axis=1,
        concat_axis=3,
        tiled=True,
    )
    ordered = returned.reshape(parts, rows_z, rows_y, size_z, size_y, width)
    ordered = jnp.swapaxes(ordered, 3, 4).reshape(parts, rows_z, rows_y, bands, length)
    return transform_axis(jnp.moveaxis(ordered, 3, 1), 4, inverse)


def apply_kinetic(field, cutoff_sq, forward, inverse):
    return slab_kinetic(field, cutoff_sq, forward, inverse)


def body(wavefunctions, potential, cutoff_sq, locked_mask):
    length = wavefunctions.shape[4]
    forward = make_tables(length, False)
    inverse = make_tables(length, True)
    blocks = wavefunctions.shape[1] // 4

    def one_block(block, result):
        piece = lax.dynamic_slice_in_dim(wavefunctions, block * 4, 4, 1)
        done = apply_kinetic(piece, cutoff_sq, forward, inverse)
        return lax.dynamic_update_slice_in_dim(result, done, block * 4, 1)

    kinetic_part = lax.fori_loop(0, blocks, one_block, jnp.zeros_like(wavefunctions))
    applied = kinetic_part + potential[None, None] * wavefunctions
    norm_local = jnp.sum(wavefunctions * wavefunctions, axis=(0, 2, 3, 4))
    correlation_local = jnp.sum(wavefunctions * applied, axis=(0, 2, 3, 4))
    norm_sq, correlation = lax.psum((norm_local, correlation_local), ("py", "pz"))
    rayleigh = correlation / norm_sq
    residual = applied - rayleigh[None, :, None, None, None] * wavefunctions
    residual_sq = lax.psum(jnp.sum(residual * residual, axis=(0, 2, 3, 4)), ("py", "pz"))
    residual_norm = jnp.sqrt(residual_sq / norm_sq) * (1.0 - locked_mask.astype(jnp.float32))
    return (applied, rayleigh, residual_norm)


def solution(mesh):
    in_specs = (P(None, None, "pz", "py", None), P("pz", "py", None), P(), P())
    out_specs = (P(None, None, "pz", "py", None), P(), P())
    return jax.shard_map(body, mesh=mesh, in_specs=in_specs, out_specs=out_specs, check_vma=False)
```

profile of v0, /device:TPU:0, one launch (start us, length us, event | category | flops | bytes accessed | tf_op | source)
XLA Modules:
  0.0 693.6 jit_solution(16688748125790381216)
XLA Ops:
  3.2 599.9 %while.18 = (s32[]{:T(128)}, f32[2,8,16,32,128]{4,3,2,1,0:T(8,128)}, f32[2,8,16,32,128]{4,3,2,1,0:T(8,128)}, s32[1]{0:T(128)}, s32[]{:T(128)}, /*index=5*/s32[]{...) while((s32[]{:T(128)}, ...), condition=%wide.region_1.2_spmd.clone.clone, body=%wide.region_0.1_spmd.clone.clone.sunk | while | flops 9676570624 | bytes 232916592 | solution.py:98
  13.3 7.5 %copy.142 = f32[2,16,32,4,128]{2,1,0,4,3:T(8,128)} copy(f32[2,16,32,4,128]{4,2,1,3,0:T(8,128)S(1)} %maximum_bitcast_fusion.2) | data formatting | bytes 4194304 | tf_op jit(solution)/shard_map/while/body/eval_jaxpr/reshape | solution.py:53
  20.7 6.1 reshape.143
  26.9 30.2 %all_to_all.204 = f32[4,1,131072]{2,1,0:T(1,128)} all-to-all(f32[4,1,131072]{2,1,0:T(1,128)S(1)} %reshape.143), channel_id=1, replica_groups=mesh['py'=4,'pz'=8] {'py'}, dimensions={0} | all-to-all | bytes 4194304 | tf_op jit(solution)/shard_map/while/body/eval_jaxpr/all_to_all | solution.py:55
  57.6 7.7 %reduce.4 = f32[4,131072]{1,0:T(4,128)S(1)} reduce(f32[4,1,131072]{2,1,0:T(1,128)} %all_to_all.204, f32[]{:T(128)} %broadcast.656), dimensions={1}, to_apply=%all_to_all.178.reduce_sub_computation | reduce | bytes 4194308 | tf_op jit(solution)/shard_map/while/body/eval_jaxpr/all_to_all | solution.py:55
  65.3 6.1 reshape.144
  71.4 5.2 copy.143
  81.3 6.9 all-to-all-start.1
  89.3 46.3 %all-to-all-done.1 = f32[2,16,128,128]{2,1,0,3:T(8,128)S(1)} async-done(((f32[2,16,128,128]{2,1,0,3:T(8,128)}), f32[2,16,128,128]{2,1,0,3:T(8,128)S(1)}, u32[]{:S(2)}, u32[]{:S(2)}) %all-to-all-start.1) | async-done | bytes 2097184 | tf_op jit(solution)/shard_map/while/body/eval_jaxpr/all_to_all | solution.py:54
  170.9 28.1 %all_to_all.205 = f32[2,128,128,16]{1,3,0,2:T(8,128)S(1)} all-to-all(f32[2,128,128,16]{1,3,0,2:T(8,128)S(1)} %copy.151), channel_id=1, replica_groups=mesh['py'=4,'pz'=8] {'py'}, dimensions={2} | all-to-all | bytes 4194304 | tf_op jit(solution)/shard_map/while/body/eval_jaxpr/all_to_all | solution.py:72
  203.8 7.2 %reshape.145 = f32[8,1,65536]{2,1,0:T(1,128)} reshape(f32[128,2,32,64]{3,2,1,0:T(8,128)} %bitcast.327) | data formatting | bytes 4194304 | tf_op jit(solution)/shard_map/while
  214.9 48.0 %all-to-all-done.3 = f32[8,1,65536]{2,1,0:T(1,128)S(1)} async-done(((f32[8,1,65536]{2,1,0:T(1,128)}), f32[8,1,65536]{2,1,0:T(1,128)S(1)}, u32[]{:S(2)}, u32[]{:S(2)}) %all-to-all-start.3) | async-done | bytes 2097184 | tf_op jit(solution)/shard_map/while/body/eval_jaxpr/all_to_all | solution.py:71
  264.8 7.2 %reduce.5 = f32[8,65536]{1,0:T(8,128)S(1)} reduce(f32[8,1,65536]{2,1,0:T(1,128)} %copy-done, f32[]{:T(128)} %broadcast.657), dimensions={1}, to_apply=%all_to_all.189.reduce_sub_computation | reduce | bytes 4194308 | tf_op jit(solution)/shard_map/while/body/eval_jaxpr/all_to_all | solution.py:71
  275.6 7.0 %copy.154 = f32[2,16,32,8,64]{2,4,3,1,0:T(8,128)} copy(f32[2,16,32,8,64]{4,2,0,1,3:T(8,128)} %bitcast.326) | data formatting | bytes 4194304 | tf_op jit(solution)/shard_map/while/body/eval_jaxpr/all_to_all | solution.py:71
  282.6 7.9 %copy.155 = f32[2,16,32,4,8,16]{2,5,4,3,1,0:T(8,128)} copy(f32[2,16,32,4,8,16]{2,5,3,4,1,0:T(8,128)} %bitcast.320) | data formatting | bytes 4194304 | tf_op jit(solution)/shard_map/while/body/eval_jaxpr/transpose | solution.py:79
  290.5 5.6 copy.156
  313.5 7.5 %copy.142 = f32[2,16,32,4,128]{2,1,0,4,3:T(8,128)} copy(f32[2,16,32,4,128]{4,2,1,3,0:T(8,128)S(1)} %maximum_bitcast_fusion.2) | data formatting | bytes 4194304 | tf_op jit(solution)/shard_map/while/body/eval_jaxpr/reshape | solution.py:53
  321.0 6.1 reshape.143
  327.2 29.1 %all_to_all.204 = f32[4,1,131072]{2,1,0:T(1,128)} all-to-all(f32[4,1,131072]{2,1,0:T(1,128)S(1)} %reshape.143), channel_id=1, replica_groups=mesh['py'=4,'pz'=8] {'py'}, dimensions={0} | all-to-all | bytes 4194304 | tf_op jit(solution)/shard_map/while/body/eval_jaxpr/all_to_all | solution.py:55
  356.8 7.7 %reduce.4 = f32[4,131072]{1,0:T(4,128)S(1)} reduce(f32[4,1,131072]{2,1,0:T(1,128)} %all_to_all.204, f32[]{:T(128)} %broadcast.656), dimensions={1}, to_apply=%all_to_all.178.reduce_sub_computation | reduce | bytes 4194308 | tf_op jit(solution)/shard_map/while/body/eval_jaxpr/all_to_all | solution.py:55
  364.5 6.1 reshape.144
  385.6 46.7 %all-to-all-done.1 = f32[2,16,128,128]{2,1,0,3:T(8,128)S(1)} async-done(((f32[2,16,128,128]{2,1,0,3:T(8,128)}), f32[2,16,128,128]{2,1,0,3:T(8,128)S(1)}, u32[]{:S(2)}, u32[]{:S(2)}) %all-to-all-start.1) | async-done | bytes 2097184 | tf_op jit(solution)/shard_map/while/body/eval_jaxpr/all_to_all | solution.py:54
  467.6 28.1 %all_to_all.205 = f32[2,128,128,16]{1,3,0,2:T(8,128)S(1)} all-to-all(f32[2,128,128,16]{1,3,0,2:T(8,128)S(1)} %copy.151), channel_id=1, replica_groups=mesh['py'=4,'pz'=8] {'py'}, dimensions={2} | all-to-all | bytes 4194304 | tf_op jit(solution)/shard_map/while/body/eval_jaxpr/all_to_all | solution.py:72
  500.5 7.2 %reshape.145 = f32[8,1,65536]{2,1,0:T(1,128)} reshape(f32[128,2,32,64]{3,2,1,0:T(8,128)} %bitcast.327) | data formatting | bytes 4194304 | tf_op jit(solution)/shard_map/while
  511.6 48.0 %all-to-all-done.3 = f32[8,1,65536]{2,1,0:T(1,128)S(1)} async-done(((f32[8,1,65536]{2,1,0:T(1,128)}), f32[8,1,65536]{2,1,0:T(1,128)S(1)}, u32[]{:S(2)}, u32[]{:S(2)}) %all-to-all-start.3) | async-done | bytes 2097184 | tf_op jit(solution)/shard_map/while/body/eval_jaxpr/all_to_all | solution.py:71
  561.5 7.2 %reduce.5 = f32[8,65536]{1,0:T(8,128)S(1)} reduce(f32[8,1,65536]{2,1,0:T(1,128)} %copy-done, f32[]{:T(128)} %broadcast.657), dimensions={1}, to_apply=%all_to_all.189.reduce_sub_computation | reduce | bytes 4194308 | tf_op jit(solution)/shard_map/while/body/eval_jaxpr/all_to_all | solution.py:71
  572.3 7.0 %copy.154 = f32[2,16,32,8,64]{2,4,3,1,0:T(8,128)} copy(f32[2,16,32,8,64]{4,2,0,1,3:T(8,128)} %bitcast.326) | data formatting | bytes 4194304 | tf_op jit(solution)/shard_map/while/body/eval_jaxpr/all_to_all | solution.py:71
  579.3 7.9 %copy.155 = f32[2,16,32,4,8,16]{2,5,4,3,1,0:T(8,128)} copy(f32[2,16,32,4,8,16]{2,5,3,4,1,0:T(8,128)} %bitcast.320) | data formatting | bytes 4194304 | tf_op jit(solution)/shard_map/while/body/eval_jaxpr/transpose | solution.py:79
  587.2 5.6 copy.156
  603.1 6.5 multiply_reduce_fusion.1
  609.6 37.5 %all-reduce = (f32[8]{0:T(128)S(1)}, f32[8]{0:T(128)S(1)}) all-reduce(f32[8]{0:T(128)S(1)} %get-tuple-element.349, f32[8]{0:T(128)S(1)} %get-tuple-element.348), channel_id=1, replica_groups=mesh['py'=4,'pz'=8] {'py','pz'}, use_global_device_ids=true, to_apply=%region_3.4 | all-reduce | flops 16 | bytes 128 | tf_op jit(solution)/shard_map/psum | solution.py:102
  651.4 41.5 %psum.23 = f32[8]{0:T(128)S(1)} all-reduce(f32[8]{0:T(128)S(1)} %multiply_reduce_fusion), channel_id=1, replica_groups=mesh['py'=4,'pz'=8] {'py','pz'}, use_global_device_ids=true, to_apply=%region_7.8 | all-reduce | flops 8 | bytes 64 | tf_op jit(solution)/shard_map/psum | solution.py:105
  (122 shorter events, 162.0 us)
Async XLA Ops:
  3.2 599.9 %copy-start.4 = (f32[16,32,128]{2,1,0:T(8,128)S(1)}, f32[16,32,128]{2,1,0:T(8,128)}, u32[]{:S(2)}) copy-start(f32[16,32,128]{2,1,0:T(8,128)} %param.7) | copy-start | bytes 786436
  81.3 54.2 %all-to-all-start.1 = ((f32[2,16,128,128]{2,1,0,3:T(8,128)}), f32[2,16,128,128]{2,1,0,3:T(8,128)S(1)}, u32[]{:S(2)}, u32[]{:S(2)}) async-start(f32[2,16,128,128]{2,1,0,3:T(8,128)} %copy.145), calls=%async_computation.1 | async-start | bytes 4194304 | tf_op jit(solution)/shard_map/while/body/eval_jaxpr/all_to_all | solution.py:54
  138.5 3.5 copy-start.1
  211.0 51.9 %all-to-all-start.3 = ((f32[8,1,65536]{2,1,0:T(1,128)}), f32[8,1,65536]{2,1,0:T(1,128)S(1)}, u32[]{:S(2)}, u32[]{:S(2)}) async-start(f32[8,1,65536]{2,1,0:T(1,128)} %reshape.145), calls=%async_computation.3 | async-start | bytes 4194304 | tf_op jit(solution)/shard_map/while/body/eval_jaxpr/all_to_all | solution.py:71
  262.9 1.4 copy-start
  298.6 2.5 copy-start.2
  301.3 2.0 copy-start.3
  380.5 51.7 %all-to-all-start.1 = ((f32[2,16,128,128]{2,1,0,3:T(8,128)}), f32[2,16,128,128]{2,1,0,3:T(8,128)S(1)}, u32[]{:S(2)}, u32[]{:S(2)}) async-start(f32[2,16,128,128]{2,1,0,3:T(8,128)} %copy.145), calls=%async_computation.1 | async-start | bytes 4194304 | tf_op jit(solution)/shard_map/while/body/eval_jaxpr/all_to_all | solution.py:54
  435.2 3.5 copy-start.1
  507.7 51.9 %all-to-all-start.3 = ((f32[8,1,65536]{2,1,0:T(1,128)}), f32[8,1,65536]{2,1,0:T(1,128)S(1)}, u32[]{:S(2)}, u32[]{:S(2)}) async-start(f32[8,1,65536]{2,1,0:T(1,128)} %reshape.145), calls=%async_computation.3 | async-start | bytes 4194304 | tf_op jit(solution)/shard_map/while/body/eval_jaxpr/all_to_all | solution.py:71
  559.6 1.4 copy-start
  595.2 2.5 copy-start.2
  598.0 2.0 copy-start.3
  647.1 4.2 copy-start.5
  647.2 45.7 %copy-start.6 = (s32[8]{0:T(128)S(1)}, s32[8]{0:T(128)}, u32[]{:S(2)}) copy-start(s32[8]{0:T(128)} %param.9) | copy-start | bytes 100
where the time goes:
time: 697 us; the launch traced here: 694 us
  blocking collectives  195 us (28%)
  waiting for transfers between devices  189 us (27%)
  local copies, waits for them, and re-layouts  156 us (22%)
  matrix products  85.4 us (12%)
  other arithmetic  44.8 us (6%)
  starting transfers between devices  18.7 us (3%)
    all_to_all x2, waiting for transfers between devices, slab_kinetic(): lax.all_to_all(lax.all_to_all(spatial, 'py', split_axis=2, concat_axis=3,...  96 us
    all_to_all x2, waiting for transfers between devices, slab_kinetic(): lax.all_to_all(lax.all_to_all(flat, 'py', split_axis=3, concat_axis=2, ti...  92.9 us
    all_to_all x2, blocking collectives, slab_kinetic(): lax.all_to_all(flat, 'py', split_axis=3, concat_axis=2, tiled=True)  59.3 us
    all_to_all x2, blocking collectives, slab_kinetic(): lax.all_to_all(spatial, 'py', split_axis=2, concat_axis=3, tiled=True)  56.3 us
    while x24, local copies, waits for them, and re-layouts  52.9 us
    psum x1, blocking collectives, body(): lax.psum(jnp.sum(residual * residual, axis=(0, 2, 3, 4)), ('py', 'pz'))  41.5 us
    psum x1, blocking collectives, body(): lax.psum((norm_local, correlation_local), ('py', 'pz'))  37.5 us
    dot_general x12, matrix products, transform_axis(): jnp.einsum(form, imag_part, sines, precision=high)  22.5 us
  transfers between devices with their start and end apart: 4, of which 4 were waited for; matrix products, arithmetic and copies ran while one was open for 0% of the time, Pallas kernels for 0%

commit v1 on v0

v1 whole, which is shorter than its diff:
```python
import math

import jax
import jax.numpy as jnp
from jax import lax
from jax.sharding import PartitionSpec as P

PREC = lax.Precision.HIGH


def make_tables(length, inverse):
    counter = jnp.arange(length, dtype=jnp.int32)
    phase = counter[:, None] * counter[None, :] % length
    angle = 2.0 * math.pi / length * phase.astype(jnp.float32)
    if inverse:
        return (jnp.cos(angle) / length, jnp.sin(angle) / length)
    return (jnp.cos(angle), -jnp.sin(angle))


def transform(form, pair, tables):
    re, im = pair
    cosines, sines = tables

    def dot(field, table):
        return jnp.einsum(form, field, table, precision=PREC)

    return (dot(re, cosines) - dot(im, sines), dot(re, sines) + dot(im, cosines))


def exchange(pair, axis, split, concat):
    return tuple(
        lax.all_to_all(part, axis, split_axis=split, concat_axis=concat, tiled=True)
        for part in pair
    )


def signed_square(counter, length):
    signed = jnp.where(counter < length // 2, counter, counter - length)
    return signed * signed


def body(wavefunctions, potential, cutoff_sq, locked_mask):
    length = wavefunctions.shape[4]
    forward = make_tables(length, False)
    inverse = make_tables(length, True)
    along_x = "bzyn,kn->bzyk"
    along_y = "bznx,kn->bzkx"
    along_z = "bnyx,kn->bkyx"
    pair = (wavefunctions[0], wavefunctions[1])
    pair = transform(along_x, pair, forward)
    pair = exchange(pair, "py", 0, 2)
    pair = transform(along_y, pair, forward)
    pair = exchange(pair, "pz", 2, 1)
    pair = transform(along_z, pair, forward)
    rows = pair[0].shape[2]
    full_sq = signed_square(jnp.arange(length, dtype=jnp.int32), length)
    own = lax.axis_index("pz") * rows + jnp.arange(rows, dtype=jnp.int32)
    own_sq = signed_square(own, length)
    total = full_sq[:, None, None] + own_sq[None, :, None] + full_sq[None, None, :]
    keep = (total <= cutoff_sq[0]).astype(jnp.float32)
    kinetic = 0.5 * (math.pi / length) ** 2 * total.astype(jnp.float32) * keep
    pair = tuple(part * kinetic[None] for part in pair)
    pair = transform(along_z, pair, inverse)
    pair = exchange(pair, "pz", 1, 2)
    pair = transform(along_y, pair, inverse)
    pair = exchange(pair, "py", 2, 0)
    pair = transform(along_x, pair, inverse)
    applied = jnp.stack(pair) + potential[None, None] * wavefunctions
    norm_own = jnp.sum(wavefunctions * wavefunctions, axis=(0, 2, 3, 4))
    corr_own = jnp.sum(wavefunctions * applied, axis=(0, 2, 3, 4))
    shift = jnp.where(norm_own > 0.0, corr_own / jnp.where(norm_own > 0.0, norm_own, 1.0), 0.0)
    rest = applied - shift[None, :, None, None, None] * wavefunctions
    rest_sq = jnp.sum(rest * rest, axis=(0, 2, 3, 4))
    rest_dot = jnp.sum(rest * wavefunctions, axis=(0, 2, 3, 4))
    sums = jnp.stack([norm_own, corr_own, shift, rest_sq, rest_dot])
    every = lax.all_gather(sums, ("py", "pz"))
    norm_all, corr_all, shift_all, sq_all, dot_all = (every[:, i] for i in range(5))
    norm_sq = jnp.sum(norm_all, axis=0)
    rayleigh = jnp.sum(corr_all, axis=0) / norm_sq
    gap = shift_all - rayleigh[None]
    residual_sq = jnp.sum(sq_all + 2.0 * gap * dot_all + gap * gap * norm_all, axis=0)
    residual_sq = jnp.maximum(residual_sq, 0.0)
    residual_norm = jnp.sqrt(residual_sq / norm_sq) * (1.0 - locked_mask.astype(jnp.float32))
    return (applied, rayleigh, residual_norm)


def solution(mesh):
    in_specs = (P(None, None, "pz", "py", None), P("pz", "py", None), P(), P())
    out_specs = (P(None, None, "pz", "py", None), P(), P())
    return jax.shard_map(body, mesh=mesh, in_specs=in_specs, out_specs=out_specs, check_vma=False)
```

time: 697 us -> 450 us (0.65)
  blocking collectives: 195 us -> 65.4 us
  local copies, waits for them, and re-layouts: 156 us -> 37.7 us
  waiting for transfers between devices: 189 us -> 251 us
  matrix products: 85.4 us -> 44.8 us
  other arithmetic: 44.8 us -> 4.45 us
  starting transfers between devices: 18.7 us -> 37.2 us
    all_to_all x4 -> x0, blocking collectives: 116 us -> none  [the longest x2 59.3 us: slab_kinetic(): lax.all_to_all(flat, 'py', split_axis=3, concat_axis=2, tiled=True)]
    psum x2 -> x0, blocking collectives: 79 us -> none  [the longest x1 41.5 us: body(): lax.psum(jnp.sum(residual * residual, axis=(0, 2, 3, 4)), ('py', 'pz'))]
    all_gather x0 -> x1, blocking collectives: none -> 65.4 us  [body(): every = lax.all_gather(sums, ('py', 'pz'))]
    all_to_all x4 -> x8, waiting for transfers between devices: 189 us -> 251 us  [exchange(): lax.all_to_all(part, axis, split_axis=split, concat_axis=concat, tiled=True)]
    while x24 -> x0, local copies, waits for them, and re-layouts: 52.9 us -> none
    dot_general x48 -> x24, matrix products: 85.4 us -> 44.8 us  [dot(): return jnp.einsum(form, field, table, precision=PREC)]
    all_to_all x4 -> x0, other arithmetic: 29.9 us -> none  [the longest x2 15.4 us: slab_kinetic(): lax.all_to_all(flat, 'py', split_axis=3, concat_axis=2, tiled=True)]
    all_to_all x18 -> x8, local copies, waits for them, and re-layouts: 47.8 us -> 18.3 us  [exchange(): lax.all_to_all(part, axis, split_axis=split, concat_axis=concat, tiled=True)]
  transfers between devices with their start and end apart: 4 -> 8, of which waited for: 4 -> 8; matrix products, arithmetic and copies ran while one was open for 0% -> 10% of each run, Pallas kernels for 0% -> 0%
where the time goes in v1:
time: 450 us; the launch traced here: 442 us
  waiting for transfers between devices  251 us (56%)
  blocking collectives  65.4 us (15%)
  matrix products  44.8 us (10%)
  local copies, waits for them, and re-layouts  37.7 us (8%)
  starting transfers between devices  37.2 us (8%)
    all_to_all x8, waiting for transfers between devices, exchange(): lax.all_to_all(part, axis, split_axis=split, concat_axis=concat, tiled=True)  251 us
    all_gather x1, blocking collectives, body(): every = lax.all_gather(sums, ('py', 'pz'))  65.4 us
    dot_general x24, matrix products, dot(): return jnp.einsum(form, field, table, precision=PREC)  44.8 us
    all_to_all x8, starting transfers between devices, exchange(): lax.all_to_all(part, axis, split_axis=split, concat_axis=concat, tiled=True)  37.2 us
    all_to_all x8, local copies, waits for them, and re-layouts, exchange(): lax.all_to_all(part, axis, split_axis=split, concat_axis=concat, tiled=True)  18.3 us
  transfers between devices with their start and end apart: 8, of which 8 were waited for; matrix products, arithmetic and copies ran while one was open for 10% of the time, Pallas kernels for 0%

profile of v1, /device:TPU:0, one launch (start us, length us, event | category | flops | bytes accessed | tf_op | source)
XLA Modules:
  0.0 442.3 jit_solution(3575044738702236548)
XLA Ops:
  0.6 3.0 fusion.8
  3.6 2.7 add_bitcast_fusion.4
  6.3 4.3 all-to-all-start.1
  10.6 3.0 fusion.10
  13.6 2.7 subtract_bitcast_fusion.4
  16.2 20.0 %all-to-all-done.1 = f32[8,16,32,128]{3,2,1,0:T(8,128)S(1)} async-done(((f32[8,16,32,128]{3,2,1,0:T(8,128)}), f32[8,16,32,128]{3,2,1,0:T(8,128)S(1)}, u32[]{:S(2)}, u32[]{:S(2)}) %all-to-all-start.1) | async-done | bytes 2097184 | tf_op jit(solution)/shard_map/all_to_all | solution.py:32
  37.6 4.5 %all-to-all-start = ((f32[8,16,32,128]{3,2,1,0:T(8,128)}), f32[8,16,32,128]{3,2,1,0:T(8,128)}, u32[]{:S(2)}, u32[]{:S(2)}) async-start(f32[8,16,32,128]{3,2,1,0:T(8,128)} %subtract_bitcast_fusion.4), calls=%async_computation | async-start | bytes 4194304 | tf_op jit(solution)/shard_map/all_to_all | solution.py:32
  43.9 23.9 %all-to-all-done = f32[8,16,32,128]{3,2,1,0:T(8,128)} async-done(((f32[8,16,32,128]{3,2,1,0:T(8,128)}), f32[8,16,32,128]{3,2,1,0:T(8,128)}, u32[]{:S(2)}, u32[]{:S(2)}) %all-to-all-start) | async-done | bytes 2097184 | tf_op jit(solution)/shard_map/all_to_all | solution.py:32
  72.2 2.5 copy.20
  74.7 6.8 %all-to-all-start.2 = ((f32[2,16,128,128]{3,1,0,2:T(8,128)}), f32[2,16,128,128]{3,1,0,2:T(8,128)}, u32[]{:S(2)}, u32[]{:S(2)}) async-start(f32[2,16,128,128]{3,1,0,2:T(8,128)} %copy.20), calls=%async_computation.2 | async-start | bytes 4194304 | tf_op jit(solution)/shard_map/all_to_all | solution.py:32
  81.6 2.8 fusion.44
  85.7 2.5 copy.22
  88.2 41.3 %all-to-all-done.2 = f32[2,16,128,128]{3,1,0,2:T(8,128)} async-done(((f32[2,16,128,128]{3,1,0,2:T(8,128)}), f32[2,16,128,128]{3,1,0,2:T(8,128)}, u32[]{:S(2)}, u32[]{:S(2)}) %all-to-all-start.2) | async-done | bytes 2097184 | tf_op jit(solution)/shard_map/all_to_all | solution.py:32
  129.5 4.3 all-to-all-start.3
  138.1 2.6 fusion.51
  140.7 41.0 %all-to-all-done.3 = f32[2,16,128,128]{3,1,0,2:T(8,128)} async-done(((f32[2,16,128,128]{3,1,0,2:T(8,128)}), f32[2,16,128,128]{3,1,0,2:T(8,128)}, u32[]{:S(2)}, u32[]{:S(2)}) %all-to-all-start.3) | async-done | bytes 2097184 | tf_op jit(solution)/shard_map/all_to_all | solution.py:32
  192.0 4.6 %all-to-all-start.4 = ((f32[2,128,16,128]{3,2,0,1:T(8,128)}), f32[2,128,16,128]{3,2,0,1:T(8,128)}, u32[]{:S(2)}, u32[]{:S(2)}) async-start(f32[2,128,16,128]{3,2,0,1:T(8,128)} %copy.24), calls=%async_computation.4 | async-start | bytes 4194304 | tf_op jit(solution)/shard_map/all_to_all | solution.py:32
  196.6 2.8 fusion
  203.2 41.2 %all-to-all-done.4 = f32[2,128,16,128]{3,2,0,1:T(8,128)} async-done(((f32[2,128,16,128]{3,2,0,1:T(8,128)}), f32[2,128,16,128]{3,2,0,1:T(8,128)}, u32[]{:S(2)}, u32[]{:S(2)}) %all-to-all-start.4) | async-done | bytes 2097184 | tf_op jit(solution)/shard_map/all_to_all | solution.py:32
  244.4 3.6 all-to-all-start.5
  248.0 3.2 copy.25
  251.2 45.2 %all-to-all-done.5 = f32[2,128,16,128]{3,2,0,1:T(8,128)S(1)} async-done(((f32[2,128,16,128]{3,2,0,1:T(8,128)}), f32[2,128,16,128]{3,2,0,1:T(8,128)S(1)}, u32[]{:S(2)}, u32[]{:S(2)}) %all-to-all-start.5) | async-done | bytes 2097184 | tf_op jit(solution)/shard_map/all_to_all | solution.py:32
  305.1 4.5 %all-to-all-start.6 = ((f32[2,16,128,128]{3,1,0,2:T(8,128)}), f32[2,16,128,128]{3,1,0,2:T(8,128)}, u32[]{:S(2)}, u32[]{:S(2)}) async-start(f32[2,16,128,128]{3,1,0,2:T(8,128)} %copy.28), calls=%async_computation.6 | async-start | bytes 4194304 | tf_op jit(solution)/shard_map/all_to_all | solution.py:32
  309.6 2.8 fusion.36
  313.7 2.5 copy.30
  316.2 19.1 %all-to-all-done.6 = f32[2,16,128,128]{3,1,0,2:T(8,128)} async-done(((f32[2,16,128,128]{3,1,0,2:T(8,128)}), f32[2,16,128,128]{3,1,0,2:T(8,128)}, u32[]{:S(2)}, u32[]{:S(2)}) %all-to-all-start.6) | async-done | bytes 2097184 | tf_op jit(solution)/shard_map/all_to_all | solution.py:32
  335.3 4.7 %all-to-all-start.7 = ((f32[2,16,128,128]{3,1,0,2:T(8,128)}), f32[2,16,128,128]{3,1,0,2:T(8,128)}, u32[]{:S(2)}, u32[]{:S(2)}) async-start(f32[2,16,128,128]{3,1,0,2:T(8,128)} %copy.30), calls=%async_computation.7 | async-start | bytes 4194304 | tf_op jit(solution)/shard_map/all_to_all | solution.py:32
  340.0 2.8 copy.29
  344.1 2.6 fusion.59
  346.6 18.9 %all-to-all-done.7 = f32[2,16,128,128]{3,1,0,2:T(8,128)} async-done(((f32[2,16,128,128]{3,1,0,2:T(8,128)}), f32[2,16,128,128]{3,1,0,2:T(8,128)}, u32[]{:S(2)}, u32[]{:S(2)}) %all-to-all-start.7) | async-done | bytes 2097184 | tf_op jit(solution)/shard_map/all_to_all | solution.py:32
  365.5 3.0 copy.31
  375.7 65.4 %all-gather.1 = f32[32,5,8]{2,1,0:T(8,128)S(1)} all-gather(f32[1,5,8]{2,1,0:T(8,128)S(1)} %bitcast.198), channel_id=2, replica_groups=mesh['py'=4,'pz'=8] {'py','pz'}, dimensions={0}, use_global_device_ids=true | all-gather | bytes 5280 | tf_op jit(solution)/shard_map/all_gather | solution.py:76
  (65 shorter events, 45.4 us)
Async XLA Ops:
  0.6 3.0 copy-start
  6.3 29.9 %all-to-all-start.1 = ((f32[8,16,32,128]{3,2,1,0:T(8,128)}), f32[8,16,32,128]{3,2,1,0:T(8,128)S(1)}, u32[]{:S(2)}, u32[]{:S(2)}) async-start(f32[8,16,32,128]{3,2,1,0:T(8,128)} %add_bitcast_fusion.4), calls=%async_computation.1 | async-start | bytes 4194304 | tf_op jit(solution)/shard_map/all_to_all | solution.py:32
  10.6 3.0 copy-start.1
  36.3 1.3 copy-start.9
  37.6 30.2 %all-to-all-start = ((f32[8,16,32,128]{3,2,1,0:T(8,128)}), f32[8,16,32,128]{3,2,1,0:T(8,128)}, u32[]{:S(2)}, u32[]{:S(2)}) async-start(f32[8,16,32,128]{3,2,1,0:T(8,128)} %subtract_bitcast_fusion.4), calls=%async_computation | async-start | bytes 4194304 | tf_op jit(solution)/shard_map/all_to_all | solution.py:32
  69.6 1.3 copy-start.5
  74.7 54.8 %all-to-all-start.2 = ((f32[2,16,128,128]{3,1,0,2:T(8,128)}), f32[2,16,128,128]{3,1,0,2:T(8,128)}, u32[]{:S(2)}, u32[]{:S(2)}) async-start(f32[2,16,128,128]{3,1,0,2:T(8,128)} %copy.20), calls=%async_computation.2 | async-start | bytes 4194304 | tf_op jit(solution)/shard_map/all_to_all | solution.py:32
  129.5 52.2 %all-to-all-start.3 = ((f32[2,16,128,128]{3,1,0,2:T(8,128)}), f32[2,16,128,128]{3,1,0,2:T(8,128)}, u32[]{:S(2)}, u32[]{:S(2)}) async-start(f32[2,16,128,128]{3,1,0,2:T(8,128)} %copy.22), calls=%async_computation.3 | async-start | bytes 4194304 | tf_op jit(solution)/shard_map/all_to_all | solution.py:32
  183.6 1.6 copy-start.7
  185.2 1.6 copy-start.3
  192.0 52.4 %all-to-all-start.4 = ((f32[2,128,16,128]{3,2,0,1:T(8,128)}), f32[2,128,16,128]{3,2,0,1:T(8,128)}, u32[]{:S(2)}, u32[]{:S(2)}) async-start(f32[2,128,16,128]{3,2,0,1:T(8,128)} %copy.24), calls=%async_computation.4 | async-start | bytes 4194304 | tf_op jit(solution)/shard_map/all_to_all | solution.py:32
  244.4 52.0 %all-to-all-start.5 = ((f32[2,128,16,128]{3,2,0,1:T(8,128)}), f32[2,128,16,128]{3,2,0,1:T(8,128)S(1)}, u32[]{:S(2)}, u32[]{:S(2)}) async-start(f32[2,128,16,128]{3,2,0,1:T(8,128)} %copy.26), calls=%async_computation.5 | async-start | bytes 4194304 | tf_op jit(solution)/shard_map/all_to_all | solution.py:32
  296.4 1.3 copy-start.10
  297.8 2.2 copy-start.4
  305.1 30.2 %all-to-all-start.6 = ((f32[2,16,128,128]{3,1,0,2:T(8,128)}), f32[2,16,128,128]{3,1,0,2:T(8,128)}, u32[]{:S(2)}, u32[]{:S(2)}) async-start(f32[2,16,128,128]{3,1,0,2:T(8,128)} %copy.28), calls=%async_computation.6 | async-start | bytes 4194304 | tf_op jit(solution)/shard_map/all_to_all | solution.py:32
  335.3 30.2 %all-to-all-start.7 = ((f32[2,16,128,128]{3,1,0,2:T(8,128)}), f32[2,16,128,128]{3,1,0,2:T(8,128)}, u32[]{:S(2)}, u32[]{:S(2)}) async-start(f32[2,16,128,128]{3,1,0,2:T(8,128)} %copy.30), calls=%async_computation.7 | async-start | bytes 4194304 | tf_op jit(solution)/shard_map/all_to_all | solution.py:32
  365.5 3.0 copy-start.8
  369.7 2.2 copy-start.2
  369.7 2.2 copy-start.11
  373.7 2.0 copy-start.6
  373.7 67.6 %copy-start.13 = (s32[8]{0:T(128)S(1)}, s32[8]{0:T(128)}, u32[]{:S(2)}) copy-start(s32[8]{0:T(128)} %param.7) | copy-start | bytes 100
  441.2 0.6 copy-start.12

commit v2 on v1

--- a/solution.py
+++ b/solution.py
@@ -1,11 +1,15 @@
+import functools
 import math
 
 import jax
 import jax.numpy as jnp
 from jax import lax
+from jax.experimental import pallas as pl
+from jax.experimental.pallas import tpu as pltpu
 from jax.sharding import PartitionSpec as P
 
-PREC = lax.Precision.HIGH
+PREC = lax.Precision.HIGHEST
+MESH = pl.DeviceIdType.MESH
 
 
 def make_tables(length, inverse):
@@ -39,10 +43,276 @@
     return signed * signed
 
 
-def body(wavefunctions, potential, cutoff_sq, locked_mask):
-    length = wavefunctions.shape[4]
-    forward = make_tables(length, False)
-    inverse = make_tables(length, True)
+def right_matrix(tables):
+    cosines, sines = tables
+    top = jnp.concatenate([cosines, sines], axis=1)
+    return jnp.concatenate([top, jnp.concatenate([-sines, cosines], axis=1)], axis=0)
+
+
+def dot(left, right):
+    return jnp.dot(left, right, precision=PREC, preferred_element_type=jnp.float32)
+
+
+def main_kernel(
+    size_y, size_z, chunks,
+    u_ref, kin_ref, xf_ref, xi_ref, lf_ref, li_ref, out_ref,
+    a1, r1, a2, r2, r3,
+    s1, q1, s2, q2, s3, q3, s4, q4,
+):
+    me_y, me_z = lax.axis_index("py"), lax.axis_index("pz")
+    _, bands, rows_z, rows_y, length = u_ref.shape
+    slots = bands // size_y
+    rows_k = length // size_z
+    step = rows_z // chunks
+    high = length
+
+    barrier = pltpu.get_barrier_semaphore()
+    for d in range(1, size_y):
+        pl.semaphore_signal(barrier, inc=1, device_id={"py": (me_y + d) % size_y}, device_id_type=MESH)
+    for d in range(1, size_z):
+        pl.semaphore_signal(barrier, inc=1, device_id={"pz": (me_z + d) % size_z}, device_id_type=MESH)
+    pl.semaphore_wait(barrier, size_y + size_z - 2)
+
+    def copy1(s, c, d):
+        to = (me_y + d) % size_y
+        return pltpu.make_async_remote_copy(
+            src_ref=a1.at[:, to * slots + s, pl.ds(c * step, step)],
+            dst_ref=r1.at[:, s, pl.ds(c * step, step), me_y],
+            send_sem=s1.at[s, c, d - 1], recv_sem=q1.at[s, c, d - 1],
+            device_id={"py": to}, device_id_type=MESH)
+
+    def copy2(s, c, d):
+        to = (me_z + d) % size_z
+        rows = step * rows_k
+        return pltpu.make_async_remote_copy(
+            src_ref=a2.at[:, s, to, pl.ds(pl.multiple_of(c * rows, rows), rows)],
+            dst_ref=r2.at[:, s, pl.ds(pl.multiple_of((me_z * chunks + c) * rows, rows), rows)],
+            send_sem=s2.at[s, c, d - 1], recv_sem=q2.at[s, c, d - 1],
+            device_id={"pz": to}, device_id_type=MESH)
+
+    def copy3(s, c, d):
+        to = (me_z + d) % size_z
+        rows = step * rows_k
+        return pltpu.make_async_remote_copy(
+            src_ref=r2.at[:, s, pl.ds(pl.multiple_of((to * chunks + c) * rows, rows), rows)],
+            dst_ref=r3.at[:, s, me_z, pl.ds(pl.multiple_of(c * rows, rows), rows)],
+            send_sem=s3.at[s, c, d - 1], recv_sem=q3.at[s, c, d - 1],
+            device_id={"pz": to}, device_id_type=MESH)
+
+    def copy4(s, c, d):
+        to = (me_y + d) % size_y
+        return pltpu.make_async_remote_copy(
+            src_ref=r1.at[:, s, pl.ds(c * step, step), to],
+            dst_ref=out_ref.at[:, me_y * slots + s, pl.ds(c * step, step)],
+            send_sem=s4.at[s, c, d - 1], recv_sem=q4.at[s, c, d - 1],
+            device_id={"py": to}, device_id_type=MESH)
+
+    order_z = sorted(range(1, size_z), key=lambda d: -min(d, size_z - d))
+
+    for s in range(slots):
+        def forward_x(c, carry):
+            for d in list(range(1, size_y)) + [0]:
+                band = (me_y + d) % size_y * slots + s
+                zs = pl.ds(c * step, step)
+                rows = jnp.concatenate(
+                    [u_ref[p, band, zs].reshape(step * rows_y, length) for p in range(2)], axis=1)
+                done = dot(rows, xf_ref[...])
+                for p in range(2):
+                    part = done[:, p * high : (p + 1) * high].reshape(step, rows_y, length)
+                    if d == 0:
+                        r1[p, s, zs, me_y] = part
+                    else:
+                        a1[p, band, zs] = part
+                if d > 0:
+                    copy1(s, c, d).start()
+            return carry
+        lax.fori_loop(0, chunks, forward_x, 0)
+
+    for s in range(slots):
+        def forward_y(c, carry):
+            for d in range(1, size_y):
+                copy1(s, c, d).wait_recv()
+            for i in range(0, step, 2):
+                sides = []
+                for z in (c * step + i, c * step + i + 1):
+                    sides.append(jnp.concatenate(
+                        [r1[p, s, z].reshape(length, length) for p in range(2)], axis=0))
+                done = dot(lf_ref[...], jnp.concatenate(sides, axis=1))
+                for p in range(2):
+                    for e in range(2):
+                        at = pl.ds(pl.multiple_of((c * step + i + e) * rows_k, rows_k), rows_k)
+                        part = done[p * high : (p + 1) * high, e * high : (e + 1) * high]
+                        a2[p, s, :, at] = part.reshape(size_z, rows_k, length)
+            for d in order_z:
+                copy2(s, c, d).start()
+            rows = step * rows_k
+            own = pl.ds(pl.multiple_of(c * rows, rows), rows)
+            r2[:, s, pl.ds(pl.multiple_of((me_z * chunks + c) * rows, rows), rows)] = a2[:, s, me_z, own]
+            return carry
+        lax.fori_loop(0, chunks, forward_y, 0)
+
+    for s in range(slots):
+        def arrive2(c, carry):
+            for d in range(1, size_z):
+                copy2(s, c, d).wait_recv()
+            return carry
+        lax.fori_loop(0, chunks, arrive2, 0)
+
+        def both_z(h, carry):
+            sides = []
+            for k in (2 * h, 2 * h + 1):
+                sides.append(jnp.concatenate(
+                    [r2[p, s, pl.ds(k, length, stride=rows_k)] for p in range(2)], axis=0))
+            spectrum = dot(lf_ref[...], jnp.concatenate(sides, axis=1))
+            weight = jnp.concatenate([kin_ref[2 * h], kin_ref[2 * h + 1]], axis=1)
+            weight = jnp.concatenate([weight, weight], axis=0)
+            done = dot(li_ref[...], spectrum * weight)
+            for p in range(2):
+                for e in range(2):
+                    r2[p, s, pl.ds(2 * h + e, length, stride=rows_k)] = done[
+                        p * high : (p + 1) * high, e * high : (e + 1) * high]
+            return carry
+        lax.fori_loop(0, rows_k // 2, both_z, 0)
+
+        def leave3(c, carry):
+            for d in order_z:
+                copy3(s, c, d).start()
+            return carry
+        lax.fori_loop(0, chunks, leave3, 0)
+        every = rows_z * rows_k
+        r3[:, s, me_z] = r2[:, s, pl.ds(pl.multiple_of(me_z * every, every), every)]
+
+    for s in range(slots):
+        def inverse_y(c, carry):
+            for d in range(1, size_z):
+                copy3(s, c, d).wait_recv()
+            for i in range(0, step, 2):
+                sides = []
+                for e in range(2):
+                    at = pl.ds(pl.multiple_of((c * step + i + e) * rows_k, rows_k), rows_k)
+                    sides.append(jnp.concatenate(
+                        [r3[p, s, :, at].reshape(length, length) for p in range(2)], axis=0))
+                done = dot(li_ref[...], jnp.concatenate(sides, axis=1))
+                for p in range(2):
+                    for e in range(2):
+                        part = done[p * high : (p + 1) * high, e * high : (e + 1) * high]
+                        r1[p, s, c * step + i + e] = part.reshape(size_y, rows_y, length)
+            for d in range(1, size_y):
+                copy4(s, c, d).start()
+            zs = pl.ds(c * step, step)
+            out_ref[:, me_y * slots + s, zs] = r1[:, s, zs, me_y]
+            return carry
+        lax.fori_loop(0, chunks, inverse_y, 0)
+
+    for s in range(slots):
+        def inverse_x(c, carry):
+            zs = pl.ds(c * step, step)
+            for d in range(size_y):
+                band = (me_y + size_y - d) % size_y * slots + s
+                if d > 0:
+                    copy4(s, c, d).wait_recv()
+                rows = jnp.concatenate(
+                    [out_ref[p, band, zs].reshape(step * rows_y, length) for p in range(2)], axis=1)
+                done = dot(rows, xi_ref[...])
+                for p in range(2):
+                    out_ref[p, band, zs] = done[:, p * high : (p + 1) * high].reshape(
+                        step, rows_y, length)
+            return carry
+        lax.fori_loop(0, chunks, inverse_x, 0)
+
+    for s in range(slots):
+        def settle(c, carry):
+            for d in range(1, size_y):
+                copy1(s, c, d).wait_send()
+                copy4(s, c, d).wait_send()
+            for d in range(1, size_z):
+                copy2(s, c, d).wait_send()
+                copy3(s, c, d).wait_send()
+            return carry
+        lax.fori_loop(0, chunks, settle, 0)
+
+
+def fused_kinetic(wavefunctions, kinetic, forward, inverse):
+    _, bands, rows_z, rows_y, length = wavefunctions.shape
+    size_y, size_z = lax.axis_size("py"), lax.axis_size("pz")
+    slots = bands // size_y
+    rows_k = length // size_z
+    chunks = rows_z // 4
+    xf, xi = right_matrix(forward), right_matrix(inverse)
+    vmem = pl.BlockSpec(memory_space=pltpu.VMEM)
+    near = pltpu.SemaphoreType.DMA((slots, chunks, size_y - 1))
+    far = pltpu.SemaphoreType.DMA((slots, chunks, size_z - 1))
+    return pl.pallas_call(
+        functools.partial(main_kernel, size_y, size_z, chunks),
+        out_shape=jax.ShapeDtypeStruct(wavefunctions.shape, jnp.float32),
+        in_specs=[vmem] * 6,
+        out_specs=vmem,
+        scratch_shapes=[
+            pltpu.VMEM((2, bands, rows_z, rows_y, length), jnp.float32),
+            pltpu.VMEM((2, slots, rows_z, size_y, rows_y, length), jnp.float32),
+            pltpu.VMEM((2, slots, size_z, rows_z * rows_k, length), jnp.float32),
+            pltpu.VMEM((2, slots, length * rows_k, length), jnp.float32),
+            pltpu.VMEM((2, slots, size_z, rows_z * rows_k, length), jnp.float32),
+            near, near, far, far, far, far, near, near,
+        ],
+        compiler_params=pltpu.CompilerParams(
+            collective_id=0, has_side_effects=True, vmem_limit_bytes=67043328),
+    )(wavefunctions, kinetic, xf, xi, xf.T, xi.T)
+
+
+def gather_kernel(size_y, size_z, own_ref, out_ref, send, recv):
+    me_y, me_z = lax.axis_index("py"), lax.axis_index("pz")
+    me = me_y * size_z + me_z
+    count = size_y * size_z
+    barrier = pltpu.get_barrier_semaphore()
+
+    def target(t):
+        to = (me + t) % count
+        return {"py": to // size_z, "pz": to % size_z}
+
+    def greet(t, carry):
+        pl.semaphore_signal(barrier, inc=1, device_id=target(t), device_id_type=MESH)
+        return carry
+    lax.fori_loop(1, count, greet, 0)
+    pl.semaphore_wait(barrier, count - 1)
+
+    def copy(t):
+        return pltpu.make_async_remote_copy(
+            src_ref=own_ref, dst_ref=out_ref.at[me], send_sem=send.at[t], recv_sem=recv.at[t],
+            device_id=target(t), device_id_type=MESH)
+
+    def leave(t, carry):
+        copy(t).start()
+        return carry
+    lax.fori_loop(1, count, leave, 0)
+    out_ref[me] = own_ref[...]
+
+    def arrive(t, carry):
+        copy(t).wait()
+        return carry
+    lax.fori_loop(1, count, arrive, 0)
+
+
+def gather_sums(sums):
+    size_y, size_z = lax.axis_size("py"), lax.axis_size("pz")
+    count = size_y * size_z
+    kinds, bands = sums.shape
+    if count > 64:
+        return lax.all_gather(sums, ("py", "pz"))
+    own = jnp.pad(sums, ((0, 8 - kinds), (0, 128 - bands)))
+    vmem = pl.BlockSpec(memory_space=pltpu.VMEM)
+    every = pl.pallas_call(
+        functools.partial(gather_kernel, size_y, size_z),
+        out_shape=jax.ShapeDtypeStruct((count, 8, 128), jnp.float32),
+        in_specs=[vmem],
+        out_specs=vmem,
+        scratch_shapes=[pltpu.SemaphoreType.DMA((count,)), pltpu.SemaphoreType.DMA((count,))],
+        compiler_params=pltpu.CompilerParams(collective_id=1, has_side_effects=True),
+    )(own)
+    return every[:, :kinds, :bands]
+
+
+def plain_kinetic(wavefunctions, kinetic, forward, inverse):
     along_x = "bzyn,kn->bzyk"
     along_y = "bznx,kn->bzkx"
     along_z = "bnyx,kn->bkyx"
@@ -52,20 +322,33 @@
     pair = transform(along_y, pair, forward)
     pair = exchange(pair, "pz", 2, 1)
     pair = transform(along_z, pair, forward)
-    rows = pair[0].shape[2]
-    full_sq = signed_square(jnp.arange(length, dtype=jnp.int32), length)
-    own = lax.axis_index("pz") * rows + jnp.arange(rows, dtype=jnp.int32)
-    own_sq = signed_square(own, length)
-    total = full_sq[:, None, None] + own_sq[None, :, None] + full_sq[None, None, :]
-    keep = (total <= cutoff_sq[0]).astype(jnp.float32)
-    kinetic = 0.5 * (math.pi / length) ** 2 * total.astype(jnp.float32) * keep
-    pair = tuple(part * kinetic[None] for part in pair)
+    pair = tuple(part * jnp.swapaxes(kinetic, 0, 1)[None] for part in pair)
     pair = transform(along_z, pair, inverse)
     pair = exchange(pair, "pz", 1, 2)
     pair = transform(along_y, pair, inverse)
     pair = exchange(pair, "py", 2, 0)
     pair = transform(along_x, pair, inverse)
-    applied = jnp.stack(pair) + potential[None, None] * wavefunctions
+    return jnp.stack(pair)
+
+
+def body(wavefunctions, potential, cutoff_sq, locked_mask):
+    length = wavefunctions.shape[4]
+    forward = make_tables(length, False)
+    inverse = make_tables(length, True)
+    size_y, size_z = lax.axis_size("py"), lax.axis_size("pz")
+    rows = length // size_z
+    full_sq = signed_square(jnp.arange(length, dtype=jnp.int32), length)
+    own = lax.axis_index("pz") * rows + jnp.arange(rows, dtype=jnp.int32)
+    own_sq = signed_square(own, length)
+    total = own_sq[:, None, None] + full_sq[None, :, None] + full_sq[None, None, :]
+    keep = (total <= cutoff_sq[0]).astype(jnp.float32)
+    kinetic = 0.5 * (math.pi / length) ** 2 * total.astype(jnp.float32) * keep
+    fits = rows % 8 == 0 and wavefunctions.shape[2] % 4 == 0 and wavefunctions.shape[1] % size_y == 0
+    if fits:
+        back = fused_kinetic(wavefunctions, kinetic, forward, inverse)
+    else:
+        back = plain_kinetic(wavefunctions, kinetic, forward, inverse)
+    applied = back + potential[None, None] * wavefunctions
     norm_own = jnp.sum(wavefunctions * wavefunctions, axis=(0, 2, 3, 4))
     corr_own = jnp.sum(wavefunctions * applied, axis=(0, 2, 3, 4))
     shift = jnp.where(norm_own > 0.0, corr_own / jnp.where(norm_own > 0.0, norm_own, 1.0), 0.0)
@@ -73,7 +356,7 @@
     rest_sq = jnp.sum(rest * rest, axis=(0, 2, 3, 4))
     rest_dot = jnp.sum(rest * wavefunctions, axis=(0, 2, 3, 4))
     sums = jnp.stack([norm_own, corr_own, shift, rest_sq, rest_dot])
-    every = lax.all_gather(sums, ("py", "pz"))
+    every = gather_sums(sums)
     norm_all, corr_all, shift_all, sq_all, dot_all = (every[:, i] for i in range(5))
     norm_sq = jnp.sum(norm_all, axis=0)
     rayleigh = jnp.sum(corr_all, axis=0) / norm_sq

time: 450 us -> 246 us (0.55); the launches traced: 442 us -> 246 us
  waiting for transfers between devices: 251 us -> 0 us
  Pallas kernels: 0 us -> 229 us
  blocking collectives: 65.4 us -> 0 us
  matrix products: 44.8 us -> 0 us
  starting transfers between devices: 37.2 us -> 0 us
  local copies, waits for them, and re-layouts: 37.7 us -> 2.68 us
  other arithmetic: 4.45 us -> 12.7 us
    all_to_all x8 -> x0, waiting for transfers between devices: 251 us -> none  [exchange(): lax.all_to_all(part, axis, split_axis=split, concat_axis=concat, tiled=True)]
    pallas_call x0 -> x2, Pallas kernels: none -> 229 us  [the longest x1 217 us: fused_kinetic(): pl.pallas_call(functools.partial(main_kernel, size_y, size_z, chunks), ou...]
    all_gather x1 -> x0, blocking collectives: 65.4 us -> none  [body(): every = lax.all_gather(sums, ('py', 'pz'))]
    dot_general x24 -> x0, matrix products: 44.8 us -> none  [dot(): return jnp.einsum(form, field, table, precision=PREC)]
    all_to_all x8 -> x0, starting transfers between devices: 37.2 us -> none  [exchange(): lax.all_to_all(part, axis, split_axis=split, concat_axis=concat, tiled=True)]
    all_to_all x8 -> x0, local copies, waits for them, and re-layouts: 18.3 us -> none  [exchange(): lax.all_to_all(part, axis, split_axis=split, concat_axis=concat, tiled=True)]
    add x3 -> x0, local copies, waits for them, and re-layouts: 7.6 us -> none  [transform(): dot(re, sines) + dot(im, cosines)]
    sub x3 -> x0, local copies, waits for them, and re-layouts: 7.6 us -> none  [transform(): dot(re, cosines) - dot(im, sines)]
  transfers between devices with their start and end apart: 8 -> 0, of which waited for: 8 -> 0; matrix products, arithmetic and copies ran while one was open for 10% -> 0% of each run, Pallas kernels for 0% -> 0%
where the time goes in v2:
time: 246 us
  Pallas kernels  229 us (93%)
  other arithmetic  12.7 us (5%)
  local copies, waits for them, and re-layouts  2.68 us (1%)
    pallas_call x1, Pallas kernels, fused_kinetic(): pl.pallas_call(functools.partial(main_kernel, size_y, size_z, chunks), ou...  217 us
    pallas_call x1, Pallas kernels, gather_sums(): pl.pallas_call(functools.partial(gather_kernel, size_y, size_z), out_shap...  11.6 us
    reduce_sum x1, other arithmetic, body(): corr_own = jnp.sum(wavefunctions * applied, axis=(0, 2, 3, 4))  5.29 us

profile of v2, /device:TPU:0, one launch (start us, length us, event | category | flops | bytes accessed | tf_op | source)
XLA Modules:
  0.0 245.7 jit_solution(11210330571527472388)
XLA Ops:
  1.3 0.1 broadcast_add_fusion
  1.4 0.3 fusion.11
  1.6 0.3 fusion.10
  1.9 0.3 fusion.8
  2.2 0.3 broadcast_multiply_fusion
  2.5 0.7 fusion.16
  3.2 0.9 copy.8.xi_ref
  4.1 0.7 fusion.17
  4.8 0.8 copy.7.xf_ref
  5.6 1.3 fusion.1.kin_ref
  6.9 217.3 %shard_map.67 = f32[2,8,16,32,128]{4,3,2,1,0:T(8,128)} custom-call(f32[2,8,16,32,128]{4,3,2,1,0:T(8,128)} %u_ref.1, f32[16,128,128]{2,1,0:T(8,128)} %fusion.1.kin_ref, f32[256,256]{1,0:T(8,128)} %copy.7.xf_ref, f32[256,256]{1,0:T(8,128)} %copy.8.xi_ref, f32[256,256]{1,0:T(8,128)} %get-tuple-element.10.lf_ref, f32[256,256]{1,0:T(8,128)} %get-tuple-element.8.li_ref), custom_call_target="tpu_custom_call" | custom-call | tf_op jit(solution)/shard_map/pallas_call | solution.py:245
  224.2 0.0 copy-start
  224.3 5.3 %multiply_reduce_fusion.2 = (f32[8]{0:T(128)S(1)}, f32[8]{0:T(128)S(1)}, f32[2,8,16,32,128]{4,3,2,1,0:T(8,128)S(1)}) fusion(f32[2,8,16,32,128]{4,3,2,1,0:T(8,128)} %u_ref.1, f32[2,8,16,32,128]{4,3,2,1,0:T(8,128)} %shard_map.67, f32[16,32,128]{2,1,0:T(8,128)} %param.5), kind=kLoop, calls=%fused_computation.3 | loop fusion | flops 6291440 | bytes 12845120 | tf_op jit(solution)/shard_map/reduce_sum | solution.py:353
  229.5 0.0 copy-start.1
  229.6 0.0 copy-done
  229.6 0.0 copy-start.3
  229.6 1.6 multiply_reduce_fusion
  231.2 0.4 copy-done.1
  231.6 0.6 pad.4.own_ref
  232.2 11.6 %shard_map.68 = f32[32,8,128]{2,1,0:T(8,128)} custom-call(f32[8,128]{1,0:T(8,128)} %pad.4.own_ref), custom_call_target="tpu_custom_call" | custom-call | tf_op jit(solution)/shard_map/pallas_call | solution.py:304
  243.8 1.3 fusion.18
  245.1 0.0 copy-start.2
  245.1 0.0 copy-done.3
  245.1 0.5 subtract_multiply_fusion
  245.7 0.0 copy-done.2
  (8 shorter events, 0.1 us)
Async XLA Ops:
  224.2 5.3 %copy-start = (f32[2,8,16,32,128]{4,3,2,1,0:T(8,128)S(1)}, f32[2,8,16,32,128]{4,3,2,1,0:T(8,128)}, u32[]{:S(2)}) copy-start(f32[2,8,16,32,128]{4,3,2,1,0:T(8,128)} %u_ref.1) | copy-start | bytes 12582916
  229.5 2.0 copy-start.1
  229.6 15.5 %copy-start.3 = (s32[8]{0:T(128)S(1)}, s32[8]{0:T(128)}, u32[]{:S(2)}) copy-start(s32[8]{0:T(128)} %param.7) | copy-start | bytes 100
  245.1 0.6 copy-start.2

commit v3 on v2

--- a/solution.py
+++ b/solution.py
@@ -3,6 +3,7 @@
 
 import jax
 import jax.numpy as jnp
+import numpy as np
 from jax import lax
 from jax.experimental import pallas as pl
 from jax.experimental.pallas import tpu as pltpu
@@ -49,20 +50,49 @@
     return jnp.concatenate([top, jnp.concatenate([-sines, cosines], axis=1)], axis=0)
 
 
+def fold_rows(length, extra):
+    half = length // 2
+    reach = {f: math.isqrt(half * half - f * f) for f in range(-half, half)}
+    guests = [f for f in sorted(reach, key=lambda f: (reach[f], f)) if f != -half][:extra]
+    free = [f for f in reach if f not in guests and f != -half]
+    hosts = []
+    for g in reversed(guests):
+        fits = [f for f in free if reach[f] + reach[g] < half]
+        if not fits:
+            return None
+        hosts.append(min(fits, key=lambda f: (abs(f), f)))
+        free.remove(hosts[-1])
+    hosts = hosts[::-1]
+    plain = [f for f in sorted(reach) if f not in hosts and f not in guests]
+    order = np.array(plain + hosts + guests)
+    lanes = np.arange(length)
+    signed = np.where(lanes < half, lanes, lanes - length)
+    moved = np.roll(signed, half)
+    mask = np.abs(signed)[None, :] <= np.array([reach[f] for f in hosts])[:, None]
+    hosts, guests = np.array(hosts), np.array(guests)
+    square = np.concatenate([
+        np.array(plain)[:, None] ** 2 + signed[None, :] ** 2,
+        np.where(mask, hosts[:, None] ** 2 + signed[None, :] ** 2,
+                 guests[:, None] ** 2 + moved[None, :] ** 2)])
+    return order % length, mask.astype(np.float32), square.astype(np.int32)
+
+
 def dot(left, right):
     return jnp.dot(left, right, precision=PREC, preferred_element_type=jnp.float32)
 
 
 def main_kernel(
     size_y, size_z, chunks,
-    u_ref, kin_ref, xf_ref, xi_ref, lf_ref, li_ref, out_ref,
+    u_ref, kin_ref, xf_ref, xi_ref, lf_ref, li_ref, yf_ref, yi_ref, mask_ref, out_ref,
     a1, r1, a2, r2, r3,
     s1, q1, s2, q2, s3, q3, s4, q4,
 ):
     me_y, me_z = lax.axis_index("py"), lax.axis_index("pz")
     _, bands, rows_z, rows_y, length = u_ref.shape
     slots = bands // size_y
-    rows_k = length // size_z
+    rows_k = kin_ref.shape[0]
+    extra = mask_ref.shape[0]
+    hosts = length - 2 * extra
     step = rows_z // chunks
     high = length
 
@@ -132,17 +162,26 @@
         def forward_y(c, carry):
             for d in range(1, size_y):
                 copy1(s, c, d).wait_recv()
+            folded = [[], []]
             for i in range(0, step, 2):
                 sides = []
                 for z in (c * step + i, c * step + i + 1):
                     sides.append(jnp.concatenate(
                         [r1[p, s, z].reshape(length, length) for p in range(2)], axis=0))
-                done = dot(lf_ref[...], jnp.concatenate(sides, axis=1))
+                done = dot(yf_ref[...], jnp.concatenate(sides, axis=1))
                 for p in range(2):
                     for e in range(2):
-                        at = pl.ds(pl.multiple_of((c * step + i + e) * rows_k, rows_k), rows_k)
                         part = done[p * high : (p + 1) * high, e * high : (e + 1) * high]
-                        a2[p, s, :, at] = part.reshape(size_z, rows_k, length)
+                        mask = mask_ref[...]
+                        guest = pltpu.roll(part[hosts + extra :], length // 2, axis=1)
+                        shared = part[hosts : hosts + extra] * mask + guest * (1.0 - mask)
+                        folded[p].append(jnp.concatenate([part[:hosts], shared], axis=0))
+            rows = step * rows_k
+            at = pl.ds(pl.multiple_of(c * rows, rows), rows)
+            for p in range(2):
+                for m in range(size_z):
+                    a2[p, s, m, at] = jnp.concatenate(
+                        [part[m * rows_k : (m + 1) * rows_k] for part in folded[p]], axis=0)
             for d in order_z:
                 copy2(s, c, d).start()
             rows = step * rows_k
@@ -186,13 +225,23 @@
         def inverse_y(c, carry):
             for d in range(1, size_z):
                 copy3(s, c, d).wait_recv()
+            rows = step * rows_k
+            at = pl.ds(pl.multiple_of(c * rows, rows), rows)
+            held = [[r3[p, s, m, at] for m in range(size_z)] for p in range(2)]
             for i in range(0, step, 2):
                 sides = []
                 for e in range(2):
-                    at = pl.ds(pl.multiple_of((c * step + i + e) * rows_k, rows_k), rows_k)
-                    sides.append(jnp.concatenate(
-                        [r3[p, s, :, at].reshape(length, length) for p in range(2)], axis=0))
-                done = dot(li_ref[...], jnp.concatenate(sides, axis=1))
+                    both = []
+                    for p in range(2):
+                        part = jnp.concatenate(
+                            [held[p][m][(i + e) * rows_k : (i + e + 1) * rows_k]
+                             for m in range(size_z)], axis=0)
+                        mask = mask_ref[...]
+                        shared = part[hosts:]
+                        guest = pltpu.roll(shared * (1.0 - mask), length // 2, axis=1)
+                        both += [part[:hosts], shared * mask, guest]
+                    sides.append(jnp.concatenate(both, axis=0))
+                done = dot(yi_ref[...], jnp.concatenate(sides, axis=1))
                 for p in range(2):
                     for e in range(2):
                         part = done[p * high : (p + 1) * high, e * high : (e + 1) * high]
@@ -232,20 +281,26 @@
         lax.fori_loop(0, chunks, settle, 0)
 
 
-def fused_kinetic(wavefunctions, kinetic, forward, inverse):
+def fused_kinetic(wavefunctions, cutoff_sq, folding, forward, inverse):
+    order, mask, square = folding
     _, bands, rows_z, rows_y, length = wavefunctions.shape
     size_y, size_z = lax.axis_size("py"), lax.axis_size("pz")
     slots = bands // size_y
-    rows_k = length // size_z
+    rows_k = square.shape[0] // size_z
     chunks = rows_z // 4
     xf, xi = right_matrix(forward), right_matrix(inverse)
+    both = np.concatenate([order, order + length])
+    own_sq = lax.dynamic_slice_in_dim(jnp.asarray(square), lax.axis_index("pz") * rows_k, rows_k, 0)
+    full_sq = signed_square(jnp.arange(length, dtype=jnp.int32), length)
+    kinetic = weigh(own_sq[:, None, :] + full_sq[None, :, None], cutoff_sq, length)
+    tables = (kinetic, xf, xi, xf.T, xi.T, xf.T[both], xi.T[:, both], jnp.asarray(mask))
     vmem = pl.BlockSpec(memory_space=pltpu.VMEM)
     near = pltpu.SemaphoreType.DMA((slots, chunks, size_y - 1))
     far = pltpu.SemaphoreType.DMA((slots, chunks, size_z - 1))
     return pl.pallas_call(
         functools.partial(main_kernel, size_y, size_z, chunks),
         out_shape=jax.ShapeDtypeStruct(wavefunctions.shape, jnp.float32),
-        in_specs=[vmem] * 6,
+        in_specs=[vmem] * 9,
         out_specs=vmem,
         scratch_shapes=[
             pltpu.VMEM((2, bands, rows_z, rows_y, length), jnp.float32),
@@ -257,7 +312,7 @@
         ],
         compiler_params=pltpu.CompilerParams(
             collective_id=0, has_side_effects=True, vmem_limit_bytes=67043328),
-    )(wavefunctions, kinetic, xf, xi, xf.T, xi.T)
+    )(wavefunctions, *tables)
 
 
 def gather_kernel(size_y, size_z, own_ref, out_ref, send, recv):
@@ -312,6 +367,11 @@
     return every[:, :kinds, :bands]
 
 
+def weigh(total, cutoff_sq, length):
+    keep = (total <= cutoff_sq[0]).astype(jnp.float32)
+    return 0.5 * (math.pi / length) ** 2 * total.astype(jnp.float32) * keep
+
+
 def plain_kinetic(wavefunctions, kinetic, forward, inverse):
     along_x = "bzyn,kn->bzyk"
     along_y = "bznx,kn->bzkx"
@@ -337,16 +397,19 @@
     inverse = make_tables(length, True)
     size_y, size_z = lax.axis_size("py"), lax.axis_size("pz")
     rows = length // size_z
-    full_sq = signed_square(jnp.arange(length, dtype=jnp.int32), length)
-    own = lax.axis_index("pz") * rows + jnp.arange(rows, dtype=jnp.int32)
-    own_sq = signed_square(own, length)
-    total = own_sq[:, None, None] + full_sq[None, :, None] + full_sq[None, None, :]
-    keep = (total <= cutoff_sq[0]).astype(jnp.float32)
-    kinetic = 0.5 * (math.pi / length) ** 2 * total.astype(jnp.float32) * keep
-    fits = rows % 8 == 0 and wavefunctions.shape[2] % 4 == 0 and wavefunctions.shape[1] % size_y == 0
-    if fits:
-        back = fused_kinetic(wavefunctions, kinetic, forward, inverse)
+    extra = 2 * size_z
+    kept = rows - 2
+    fits = extra % 8 == 0 and 4 * kept % 8 == 0 and kept > 2 and rows % 8 == 0
+    fits = fits and wavefunctions.shape[2] % 4 == 0 and wavefunctions.shape[1] % size_y == 0
+    folding = fold_rows(length, extra) if fits else None
+    if folding is not None:
+        back = fused_kinetic(wavefunctions, cutoff_sq, folding, forward, inverse)
     else:
+        full_sq = signed_square(jnp.arange(length, dtype=jnp.int32), length)
+        own = lax.axis_index("pz") * rows + jnp.arange(rows, dtype=jnp.int32)
+        own_sq = signed_square(own, length)
+        total = own_sq[:, None, None] + full_sq[None, :, None] + full_sq[None, None, :]
+        kinetic = weigh(total, cutoff_sq, length)
         back = plain_kinetic(wavefunctions, kinetic, forward, inverse)
     applied = back + potential[None, None] * wavefunctions
     norm_own = jnp.sum(wavefunctions * wavefunctions, axis=(0, 2, 3, 4))

time: 246 us -> 227 us (0.923)
  Pallas kernels: 229 us -> 207 us
  local copies, waits for them, and re-layouts: 2.68 us -> 6.99 us
    pallas_call x1, Pallas kernels: 217 us -> 195 us  [fused_kinetic(): pl.pallas_call(functools.partial(main_kernel, size_y, size_z, chunks), ou...]
    gather x0 -> x3, local copies, waits for them, and re-layouts: none -> 3.49 us  [the longest x2 1.82 us: fused_kinetic(): xi.T[:, both]]
where the time goes in v3:
time: 227 us
  Pallas kernels  207 us (91%)
  other arithmetic  11.8 us (5%)
  local copies, waits for them, and re-layouts  6.99 us (3%)
    pallas_call x1, Pallas kernels, fused_kinetic(): pl.pallas_call(functools.partial(main_kernel, size_y, size_z, chunks), ou...  195 us
    pallas_call x1, Pallas kernels, gather_sums(): pl.pallas_call(functools.partial(gather_kernel, size_y, size_z), out_shap...  11.2 us
    reduce_sum x1, other arithmetic, body(): corr_own = jnp.sum(wavefunctions * applied, axis=(0, 2, 3, 4))  5.29 us

profile of v3, /device:TPU:0, one launch (start us, length us, event | category | flops | bytes accessed | tf_op | source)
XLA Modules:
  0.0 226.7 jit_solution(1218377258146025458)
XLA Ops:
  1.3 0.7 pad_clamp_fusion
  2.0 0.7 constant_dynamic-slice_fusion
  2.7 0.3 fusion.11
  3.0 0.3 fusion.10
  3.2 0.3 fusion.8
  3.5 0.3 broadcast_multiply_fusion
  3.8 0.0 copy-start.3
  3.8 0.8 copy.15.xi_ref
  4.7 0.1 copy.12
  4.8 1.0 gather_fusion.1
  5.8 0.9 copy.13
  6.7 0.0 copy-start.1
  6.7 0.8 copy.14.xf_ref
  7.5 0.0 copy-done.1
  7.5 1.7 gather_fusion
  9.2 0.0 copy-done.3
  9.2 1.1 fusion.1.kin_ref
  10.3 195.4 %shard_map.112 = f32[2,8,16,32,128]{4,3,2,1,0:T(8,128)} custom-call(f32[2,8,16,32,128]{4,3,2,1,0:T(8,128)} %u_ref.1, f32[14,128,128]{2,1,0:T(8,128)} %fusion.1.kin_ref, f32[256,256]{1,0:T(8,128)} %copy.14.xf_ref, f32[256,256]{1,0:T(8,128)} %copy.15.xi_ref, f32[256,256]{1,0:T(8,128)} %copy-done.1, f32[256,256]{1,0:T(8,128)} %copy-done.3, ...), custom_call_target="tpu_custom_call" | custom-call | tf_op jit(solution)/shard_map/pallas_call | solution.py:300
  205.7 0.0 copy-start
  205.7 5.3 %multiply_reduce_fusion.2 = (f32[8]{0:T(128)S(1)}, f32[8]{0:T(128)S(1)}, f32[2,8,16,32,128]{4,3,2,1,0:T(8,128)S(1)}) fusion(f32[2,8,16,32,128]{4,3,2,1,0:T(8,128)} %u_ref.1, f32[2,8,16,32,128]{4,3,2,1,0:T(8,128)} %shard_map.112, f32[16,32,128]{2,1,0:T(8,128)} %param.10), kind=kLoop, calls=%fused_computation.5 | loop fusion | flops 6291440 | bytes 12845120 | tf_op jit(solution)/shard_map/reduce_sum | solution.py:416
  211.0 0.0 copy-start.2
  211.0 0.0 copy-done
  211.1 0.0 copy-start.5
  211.1 1.6 multiply_reduce_fusion
  212.7 0.4 copy-done.2
  213.1 0.6 pad.4.own_ref
  213.6 11.2 %shard_map.113 = f32[32,8,128]{2,1,0:T(8,128)} custom-call(f32[8,128]{1,0:T(8,128)} %pad.4.own_ref), custom_call_target="tpu_custom_call" | custom-call | tf_op jit(solution)/shard_map/pallas_call | solution.py:359
  224.8 1.3 fusion.17
  226.1 0.0 copy-start.4
  226.2 0.0 copy-done.5
  226.2 0.5 subtract_multiply_fusion
  226.7 0.0 copy-done.4
  (9 shorter events, 0.2 us)
Async XLA Ops:
  3.8 5.4 %copy-start.3 = (f32[256,256]{1,0:T(8,128)}, f32[256,256]{1,0:T(8,128)S(1)}, u32[]{:S(2)}) copy-start(f32[256,256]{1,0:T(8,128)S(1)} %get-tuple-element.8.li_ref) | copy-start | bytes 786436
  6.7 0.8 copy-start.1
  205.7 5.3 %copy-start = (f32[2,8,16,32,128]{4,3,2,1,0:T(8,128)S(1)}, f32[2,8,16,32,128]{4,3,2,1,0:T(8,128)}, u32[]{:S(2)}) copy-start(f32[2,8,16,32,128]{4,3,2,1,0:T(8,128)} %u_ref.1) | copy-start | bytes 12582916
  211.0 2.0 copy-start.2
  211.1 15.1 %copy-start.5 = (s32[8]{0:T(128)S(1)}, s32[8]{0:T(128)}, u32[]{:S(2)}) copy-start(s32[8]{0:T(128)} %param.12) | copy-start | bytes 100
  226.1 0.6 copy-start.4
